TPU v7x, 32 devices: a whole 2x2x4 slice. The times are simulated.
32 devices in a mesh: aa: 4 (over z), ba: 8 (over y, x, core).
Axes of the slice: x: 2, y: 2, z: 4, core: 2. Of those that a mesh axis runs over, the one named last changes fastest.
Arguments:
- grad_out: bfloat16 [4096, 4096], P('aa', 'ba')
- saved_input: bfloat16 [4096, 4096], P(('aa', 'ba'))
- keep_bits: int32 [4096, 128], P(('aa', 'ba')), may hold values from -2147483648 to 2147483647, as said below
- gain: float32 [4096], replicated, may hold values from 0.5 to 1.5
Outputs:
- grad_in: bfloat16 [4096, 4096], P(('aa', 'ba'))
- gain_grad: float32 [4096], P('ba')
Inputs may be any that keep to these rules, and one draw needn't show every extreme that they name: `keep_bits`: bit k of word w in row t (bit 31 being the sign bit) is the keep flag of feature 32 * w + k of token t; about nine in ten flags are 1.
All inputs are finite; a program needn't handle non-finite values.
Results may differ from a plain program's by a relative error of at most 0.001.
Values may be sent and summed in bfloat16 or wider, within the bound.
A program may use at most 64 MiB of HBM per device.

v0:
```python
import math

import jax
import jax.numpy as jnp
from jax import lax
from jax.sharding import PartitionSpec as P

KEEP_RATE = 0.9
EPSILON = 1e-06


def unpack_bits(words):
    shifts = jnp.arange(32, dtype=jnp.int32)
    bits = jnp.right_shift(words[:, :, None], shifts[None, None, :]) & 1
    return bits.reshape(words.shape[0], words.shape[1] * 32).astype(jnp.float32)


def rows_backward(grad_rows, input_rows, word_rows, gain):
    keep = unpack_bits(word_rows)
    dropped = input_rows.astype(jnp.float32) * keep * (1.0 / KEEP_RATE)
    inverse = lax.rsqrt(jnp.mean(dropped * dropped, axis=-1, keepdims=True) + EPSILON)
    normed = dropped * inverse
    grads = grad_rows.astype(jnp.float32)
    scaled = gain[None, :] * grads
    centre = jnp.mean(scaled * normed, axis=-1, keepdims=True)
    grad_in = (inverse * (scaled - normed * centre) * keep * (1.0 / KEEP_RATE)).astype(jnp.bfloat16)
    partial_sum = jnp.sum(grads * normed, axis=0)
    return (grad_in, partial_sum)


def per_device(grad_out, saved_input, keep_bits, gain):
    groups = lax.axis_size("ba")
    rows = grad_out.shape[0] // groups
    pieces = grad_out.reshape(groups, rows, grad_out.shape[1])
    arrived = lax.all_to_all(pieces, "ba", split_axis=0, concat_axis=2, tiled=True)
    grad_rows = arrived.reshape(rows, arrived.shape[2])
    grad_in, partial_sum = rows_backward(grad_rows, saved_input, keep_bits, gain)
    total_tokens = rows * groups * lax.axis_size("aa")
    owned = lax.psum_scatter(partial_sum, "ba", scatter_dimension=0, tiled=True)
    share = lax.psum(owned, "aa")
    gain_grad = share * (1.0 / math.sqrt(total_tokens))
    return (grad_in, gain_grad)


def solution(mesh):
    placed = (P("aa", "ba"), P(("aa", "ba"), None), P(("aa", "ba"), None), P())
    return jax.shard_map(
        per_device,
        mesh=mesh,
        in_specs=placed,
        out_specs=(P(("aa", "ba"), None), P("ba")),
        check_vma=False,
    )
```

profile of v0, /device:TPU:0, one launch (start us, length us, event | category | flops | bytes accessed | tf_op | source)
XLA Modules:
  0.0 63.3 jit_solution(16669645412910738614)
XLA Ops:
  0.6 2.3 %copy.13 = bf16[8,128,512]{1,2,0:T(8,128)(2,1)} copy(bf16[8,128,512]{2,1,0:T(8,128)(2,1)} %bitcast.48) | data formatting | bytes 2097152 | tf_op jit(solution)/shard_map/reshape | solution.py:34
  2.9 0.0 copy-start
  2.9 5.3 %all-to-all-start = ((bf16[8,128,512]{1,2,0:T(8,128)(2,1)}), bf16[8,128,512]{1,2,0:T(8,128)(2,1)S(1)}, u32[]{:S(2)}, u32[]{:S(2)}) async-start(bf16[8,128,512]{1,2,0:T(8,128)(2,1)} %copy.13), calls=%async_computation | async-start | bytes 2097152 | tf_op jit(solution)/shard_map/all_to_all | solution.py:35
  8.2 0.0 copy-done
  8.2 0.0 copy-start.2
  8.2 0.0 copy-start.3
  8.3 0.7 %copy.11 = bf16[128,4096]{0,1:T(8,128)(2,1)S(1)} copy(bf16[128,4096]{1,0:T(8,128)(2,1)S(1)} %copy-done) | data formatting | bytes 2097152 | tf_op args[1]
  8.9 0.0 copy-start.1
  9.0 0.1 shift_right_arithmetic.23
  9.0 0.0 copy-done.2
  9.1 0.1 copy.12
  9.2 0.0 copy-done.3
  9.2 0.6 dynamic-slice
  10.4 0.7 %multiply_reduce_fusion = f32[128]{0:T(128)S(1)} fusion(bf16[128,4096]{0,1:T(8,128)(2,1)S(1)} %copy.11, s32[4096]{0:T(1024)S(1)} %shift_right_arithmetic.23, s32[128,128]{0,1:T(8,128)S(1)} %copy.12), kind=kLoop, calls=%fused_computation.14 | loop fusion | flops 4194176 | bytes 1131008 | tf_op jit(solution)/shard_map/reduce_sum | solution.py:21
  11.2 12.4 %all-to-all-done = bf16[8,128,512]{1,2,0:T(8,128)(2,1)S(1)} async-done(((bf16[8,128,512]{1,2,0:T(8,128)(2,1)}), bf16[8,128,512]{1,2,0:T(8,128)(2,1)S(1)}, u32[]{:S(2)}, u32[]{:S(2)}) %all-to-all-start) | async-done | bytes 1048608 | tf_op jit(solution)/shard_map/all_to_all | solution.py:35
  23.6 0.0 copy-done.1
  23.6 2.0 %fusion.7 = (f32[4096]{0:T(1024)S(1)}, f32[128]{0:T(128)S(1)}) fusion(bf16[128,4096]{0,1:T(8,128)(2,1)S(1)} %copy.11, bf16[8,128,512]{1,2,0:T(8,128)(2,1)S(1)} %all-to-all-done, f32[128]{0:T(128)S(1)} %get-tuple-element.9, s32[4096]{0:T(1024)S(1)} %shift_right_arithmetic.23, s32[128,128]{0,1:T(8,128)S(1)} %copy.12, f32[4096]{0:T(1024)S(1)} %copy-done.1), kind=kLoop, calls=%fused_computation.9 | loop fusion | flops 6287232 | bytes 2212864 | tf_op jit(solution)/shard_map/reduce_sum | solution.py:27
  25.6 1.4 %fusion.6 = bf16[128,4096]{0,1:T(8,128)(2,1)S(1)} fusion(bf16[128,4096]{0,1:T(8,128)(2,1)S(1)} %copy.11, bf16[8,128,512]{1,2,0:T(8,128)(2,1)S(1)} %all-to-all-done, f32[128]{0:T(128)S(1)} %broadcast_multiply_fusion.2, f32[128]{0:T(128)S(1)} %get-tuple-element.9, f32[4096]{0:T(1024)S(1)} %copy-done.1, f32[128]{0:T(128)S(1)} %get-tuple-element.8, ...), kind=kLoop, calls=%fused_computation.8 | loop fusion | flops 7340032 | bytes 3245568 | tf_op jit(solution)/shard_map/convert_element_type | solution.py:26
  27.1 1.3 %copy.14 = bf16[128,4096]{1,0:T(8,128)(2,1)} copy(bf16[128,4096]{0,1:T(8,128)(2,1)S(1)} %fusion.6) | data formatting | bytes 2097152
  28.4 22.3 %all-reduce = f32[4096]{0:T(1024)S(1)} all-reduce(f32[4096]{0:T(1024)S(1)} %get-tuple-element.6), channel_id=2, replica_groups=mesh['aa'=4,'ba'=8] {'ba'}, use_global_device_ids=true, to_apply=%region_3.0.clone | all-reduce | flops 4096 | bytes 32768
  50.7 0.1 dynamic-slice.1
  50.8 11.9 %psum.7 = f32[512]{0:T(512)S(1)} all-reduce(f32[512]{0:T(512)S(1)} %dynamic-slice.1), channel_id=1, replica_groups=mesh['aa'=4,'ba'=8] {'aa'}, use_global_device_ids=true, to_apply=%region_4.0 | all-reduce | flops 512 | bytes 4096 | tf_op jit(solution)/shard_map/psum | solution.py:40
  62.7 0.6 broadcast_multiply_fusion
  (3 shorter events, 0.0 us)
Async XLA Ops:
  2.9 5.3 %copy-start = (bf16[128,4096]{1,0:T(8,128)(2,1)S(1)}, bf16[128,4096]{1,0:T(8,128)(2,1)}, u32[]{:S(2)}) copy-start(bf16[128,4096]{1,0:T(8,128)(2,1)} %param.5) | copy-start | bytes 3145732
  2.9 20.7 %all-to-all-start = ((bf16[8,128,512]{1,2,0:T(8,128)(2,1)}), bf16[8,128,512]{1,2,0:T(8,128)(2,1)S(1)}, u32[]{:S(2)}, u32[]{:S(2)}) async-start(bf16[8,128,512]{1,2,0:T(8,128)(2,1)} %copy.13), calls=%async_computation | async-start | bytes 2097152 | tf_op jit(solution)/shard_map/all_to_all | solution.py:35
  8.2 0.8 %copy-start.2 = (s32[128,128]{1,0:T(8,128)S(1)}, s32[128,128]{1,0:T(8,128)}, u32[]{:S(2)}) copy-start(s32[128,128]{1,0:T(8,128)} %param.6) | copy-start | bytes 196612
  8.2 0.9 %copy-start.3 = (u32[32]{0:T(128)S(1)}, u32[32]{0:T(128)}, u32[]{:S(2)}) copy-start(u32[32]{0:T(128)} %constant.16) | copy-start | bytes 388
  8.9 14.7 %copy-start.1 = (f32[4096]{0:T(1024)S(1)}, f32[4096]{0:T(1024)}, u32[]{:S(2)}) copy-start(f32[4096]{0:T(1024)} %param.7) | copy-start | bytes 49156
where the time goes:
time: 63.6 us; the launch traced here: 63.3 us
  blocking collectives  34.2 us (54%)
  waiting for transfers between devices  12.4 us (19%)
  starting transfers between devices  5.33 us (8%)
  local copies, waits for them, and re-layouts  5.13 us (8%)
  other arithmetic  4.78 us (8%)
  between operations  1.38 us (2%)
    unnamed x1, blocking collectives  22.3 us
    all_to_all x1, waiting for transfers between devices, per_device(): lax.all_to_all(pieces, 'ba', split_axis=0, concat_axis=2, tiled=True)  12.4 us
    psum x1, blocking collectives, per_device(): share = lax.psum(owned, 'aa')  11.9 us
    all_to_all x1, starting transfers between devices, per_device(): lax.all_to_all(pieces, 'ba', split_axis=0, concat_axis=2, tiled=True)  5.33 us
    unnamed x13, local copies, waits for them, and re-layouts  2.78 us
    reshape x1, local copies, waits for them, and re-layouts, per_device(): pieces = grad_out.reshape(groups, rows, grad_out.shape[1])  2.26 us
    reduce_sum x1, other arithmetic, rows_backward(): partial_sum = jnp.sum(grads * normed, axis=0)  2.02 us
    convert_element_type x1, other arithmetic, rows_backward(): (inverse * (scaled - normed * centre) * keep * (1.0 / KEEP_RATE)).astype(...  1.43 us
  transfers between devices with their start and end apart: 1, of which 1 were waited for; matrix products, arithmetic and copies ran while one was open for 3% of the time, Pallas kernels for 0%

commit v1 on v0

--- a/solution.py
+++ b/solution.py
@@ -1,12 +1,18 @@
+import functools
 import math
 
 import jax
 import jax.numpy as jnp
 from jax import lax
+from jax.experimental import pallas as pl
+from jax.experimental.pallas import tpu as pltpu
 from jax.sharding import PartitionSpec as P
 
 KEEP_RATE = 0.9
 EPSILON = 1e-06
+LANES = 128
+CHUNK_ROWS = 32
+MESH = pl.DeviceIdType.MESH
 
 
 def unpack_bits(words):
@@ -28,7 +34,7 @@
     return (grad_in, partial_sum)
 
 
-def per_device(grad_out, saved_input, keep_bits, gain):
+def plain(grad_out, saved_input, keep_bits, gain):
     groups = lax.axis_size("ba")
     rows = grad_out.shape[0] // groups
     pieces = grad_out.reshape(groups, rows, grad_out.shape[1])
@@ -42,6 +48,246 @@
     return (grad_in, gain_grad)
 
 
+def kernel(n_ba, n_aa, grad_hbm, input_hbm, bits_hbm, gain_hbm, out_ref, share_ref,
+           arrived, held, words, gain_ref, normed, masked_gain, outer, sums,
+           parts, slices, shares, send_sem, recv_sem, own_sem, load_sem,
+           part_send, part_recv, share_send, share_recv):
+    ba, aa = lax.axis_index("ba"), lax.axis_index("aa")
+    rows, width = arrived.shape[1], arrived.shape[2]
+    depth = n_ba * width
+    chunks = rows // CHUNK_ROWS
+    tiles = width // LANES
+    power = n_ba & (n_ba - 1) == 0
+
+    def ba_peer(step):
+        return ba ^ step if power else lax.rem(ba + step, n_ba)
+
+    def ba_source(step):
+        return ba ^ step if power else lax.rem(ba + n_ba - step, n_ba)
+
+    def aa_peer(step):
+        return lax.rem(aa + step, n_aa)
+
+    def piece(chunk, step):
+        peer = ba_peer(step)
+        first = pl.multiple_of(peer * rows + chunk * CHUNK_ROWS, CHUNK_ROWS)
+        return pltpu.make_async_remote_copy(
+            src_ref=grad_hbm.at[pl.ds(first, CHUNK_ROWS)],
+            dst_ref=arrived.at[ba, pl.ds(chunk * CHUNK_ROWS, CHUNK_ROWS)],
+            send_sem=send_sem.at[chunk, step],
+            recv_sem=recv_sem.at[chunk, step],
+            device_id={"ba": peer},
+            device_id_type=MESH,
+        )
+
+    barrier = pltpu.get_barrier_semaphore()
+    for step in range(1, n_ba):
+        pl.semaphore_signal(barrier, inc=1, device_id={"ba": ba_peer(step)}, device_id_type=MESH)
+    for step in range(1, n_aa):
+        pl.semaphore_signal(barrier, inc=1, device_id={"aa": aa_peer(step)}, device_id_type=MESH)
+    loads = [
+        pltpu.make_async_copy(bits_hbm, words, load_sem.at[0]),
+        pltpu.make_async_copy(gain_hbm, gain_ref, load_sem.at[1]),
+        pltpu.make_async_copy(input_hbm, held, load_sem.at[2]),
+    ]
+    own = pltpu.make_async_copy(
+        grad_hbm.at[pl.ds(pl.multiple_of(ba * rows, CHUNK_ROWS), rows)], arrived.at[ba], own_sem
+    )
+    for load in loads:
+        load.start()
+    own.start()
+    pl.semaphore_wait(barrier, n_ba + n_aa - 2)
+    for chunk in range(chunks):
+        for step in reversed(range(1, n_ba)):
+            piece(chunk, step).start()
+    for load in loads:
+        load.wait()
+
+    lane = lax.broadcasted_iota(jnp.int32, (CHUNK_ROWS, LANES), 1)
+    word_of = lane // 32
+    flag = jnp.left_shift(jnp.int32(1), lane % 32)
+
+    def span(source, tile):
+        return pl.ds(pl.multiple_of(source * width + tile * LANES, LANES), LANES)
+
+    def prepare(chunk, carry):
+        block = pl.ds(pl.multiple_of(chunk * CHUNK_ROWS, CHUNK_ROWS), CHUNK_ROWS)
+
+        def drop(source, squares):
+            row_words = words[block, :]
+            for tile in range(tiles):
+                at = span(source, tile)
+                index = word_of + (source * tiles + tile) * (LANES // 32)
+                spread = jnp.take_along_axis(row_words, index, axis=1, mode="promise_in_bounds")
+                kept = (spread & flag) != 0
+                dropped = jnp.where(kept, held[block, at].astype(jnp.float32), 0.0) * (1.0 / KEEP_RATE)
+                normed[block, at] = dropped
+                masked_gain[block, at] = jnp.where(kept, gain_ref[:, at], 0.0)
+                squares = squares + dropped * dropped
+            return squares
+
+        squares = lax.fori_loop(0, n_ba, drop, jnp.zeros((CHUNK_ROWS, LANES), jnp.float32))
+        mean = jnp.sum(squares, axis=1, keepdims=True) * (1.0 / depth)
+        inverse = lax.rsqrt(mean + EPSILON)
+        outer[block, :] = jnp.broadcast_to(inverse * (1.0 / KEEP_RATE), (CHUNK_ROWS, LANES))
+
+        def scale(source, none):
+            for tile in range(tiles):
+                at = span(source, tile)
+                normed[block, at] = normed[block, at] * inverse
+            return none
+
+        lax.fori_loop(0, n_ba, scale, 0)
+        return carry
+
+    lax.fori_loop(0, chunks, prepare, 0)
+    sums[...] = jnp.zeros_like(sums)
+    own.wait()
+
+    def arrive(chunk):
+        block = pl.ds(pl.multiple_of(chunk * CHUNK_ROWS, CHUNK_ROWS), CHUNK_ROWS)
+        for step in reversed(range(1, n_ba)):
+            pltpu.make_async_remote_copy(
+                src_ref=grad_hbm.at[pl.ds(0, CHUNK_ROWS)],
+                dst_ref=arrived.at[ba_source(step), block],
+                send_sem=send_sem.at[chunk, step],
+                recv_sem=recv_sem.at[chunk, step],
+                device_id={"ba": ba_peer(step)},
+                device_id_type=MESH,
+            ).wait_recv()
+
+        def first(source, total):
+            for tile in range(tiles):
+                at = span(source, tile)
+                grads = arrived[source, block, tile * LANES:(tile + 1) * LANES].astype(jnp.float32)
+                product = grads * normed[block, at]
+                total = total + product * gain_ref[:, at]
+                sums[:, at] += jnp.sum(product.reshape(CHUNK_ROWS // 8, 8, LANES), axis=0)
+            return total
+
+        total = lax.fori_loop(0, n_ba, first, jnp.zeros((CHUNK_ROWS, LANES), jnp.float32))
+        return jnp.sum(total, axis=1, keepdims=True) * (1.0 / depth)
+
+    def finish(chunk, centre):
+        block = pl.ds(pl.multiple_of(chunk * CHUNK_ROWS, CHUNK_ROWS), CHUNK_ROWS)
+        factor = outer[block, :]
+
+        def last(source, none):
+            for tile in range(tiles):
+                at = span(source, tile)
+                grads = arrived[source, block, tile * LANES:(tile + 1) * LANES].astype(jnp.float32)
+                value = factor * (masked_gain[block, at] * grads - normed[block, at] * centre)
+                out_ref[block, at] = value.astype(jnp.bfloat16)
+            return none
+
+        lax.fori_loop(0, n_ba, last, 0)
+
+    def middle(chunk, carry):
+        finish(chunk, arrive(chunk))
+        return carry
+
+    lax.fori_loop(0, chunks - 1, middle, 0)
+    centre = arrive(chunks - 1)
+    for owner in range(n_ba):
+        parts[owner] = jnp.sum(sums[:, owner * width:(owner + 1) * width], axis=0, keepdims=True)
+
+    def part(step):
+        return pltpu.make_async_remote_copy(
+            src_ref=parts.at[ba_peer(step)],
+            dst_ref=slices.at[ba],
+            send_sem=part_send.at[step],
+            recv_sem=part_recv.at[step],
+            device_id={"ba": ba_peer(step)},
+            device_id_type=MESH,
+        )
+
+    for step in reversed(range(1, n_ba)):
+        part(step).start()
+    slices[ba] = parts[ba]
+    finish(chunks - 1, centre)
+    for step in reversed(range(1, n_ba)):
+        pltpu.make_async_remote_copy(
+            src_ref=parts.at[0], dst_ref=slices.at[ba_source(step)],
+            send_sem=part_send.at[step], recv_sem=part_recv.at[step],
+            device_id={"ba": ba_peer(step)}, device_id_type=MESH,
+        ).wait_recv()
+    total = slices[0]
+    for source in range(1, n_ba):
+        total = total + slices[source]
+    shares[aa] = total
+
+    def share(step, slot):
+        return pltpu.make_async_remote_copy(
+            src_ref=shares.at[aa], dst_ref=shares.at[slot],
+            send_sem=share_send.at[step], recv_sem=share_recv.at[step],
+            device_id={"aa": aa_peer(step)}, device_id_type=MESH,
+        )
+
+    for step in range(1, n_aa):
+        share(step, aa).start()
+    for chunk in range(chunks):
+        for step in range(1, n_ba):
+            piece(chunk, step).wait_send()
+    for step in range(1, n_ba):
+        part(step).wait_send()
+    for step in range(1, n_aa):
+        share(step, lax.rem(aa + n_aa - step, n_aa)).wait_recv()
+    total = shares[0]
+    for source in range(1, n_aa):
+        total = total + shares[source]
+    share_ref[...] = total * (1.0 / math.sqrt(rows * n_ba * n_aa))
+    for step in range(1, n_aa):
+        share(step, aa).wait_send()
+
+
+def fused(grad_out, saved_input, keep_bits, gain):
+    n_ba, n_aa = lax.axis_size("ba"), lax.axis_size("aa")
+    width = grad_out.shape[1]
+    rows, depth = saved_input.shape
+    chunks = rows // CHUNK_ROWS
+    f32 = jnp.float32
+    grad_in, share = pl.pallas_call(
+        functools.partial(kernel, n_ba, n_aa),
+        out_shape=(
+            jax.ShapeDtypeStruct((rows, depth), jnp.bfloat16),
+            jax.ShapeDtypeStruct((1, width), f32),
+        ),
+        in_specs=[pl.BlockSpec(memory_space=pl.ANY)] * 4,
+        out_specs=(pl.BlockSpec(memory_space=pltpu.VMEM), pl.BlockSpec(memory_space=pltpu.VMEM)),
+        scratch_shapes=[
+            pltpu.VMEM((n_ba, rows, width), jnp.bfloat16),
+            pltpu.VMEM((rows, depth), jnp.bfloat16),
+            pltpu.VMEM(keep_bits.shape, jnp.int32),
+            pltpu.VMEM((1, depth), f32),
+            pltpu.VMEM((rows, depth), f32),
+            pltpu.VMEM((rows, depth), f32),
+            pltpu.VMEM((rows, LANES), f32),
+            pltpu.VMEM((8, depth), f32),
+            pltpu.VMEM((n_ba, 1, width), f32),
+            pltpu.VMEM((n_ba, 1, width), f32),
+            pltpu.VMEM((n_aa, 1, width), f32),
+            pltpu.SemaphoreType.DMA((chunks, n_ba)),
+            pltpu.SemaphoreType.DMA((chunks, n_ba)),
+            pltpu.SemaphoreType.DMA,
+            pltpu.SemaphoreType.DMA((3,)),
+            pltpu.SemaphoreType.DMA((n_ba,)),
+            pltpu.SemaphoreType.DMA((n_ba,)),
+            pltpu.SemaphoreType.DMA((n_aa,)),
+            pltpu.SemaphoreType.DMA((n_aa,)),
+        ],
+        compiler_params=pltpu.CompilerParams(collective_id=0, has_side_effects=True),
+        name="regroup_backward",
+    )(grad_out, saved_input, keep_bits, gain.reshape(1, depth))
+    return (grad_in, share.reshape(width))
+
+
+def per_device(grad_out, saved_input, keep_bits, gain):
+    fits = grad_out.shape[1] % LANES == 0 and saved_input.shape[0] % CHUNK_ROWS == 0
+    fits = fits and keep_bits.shape[1] == LANES
+    body = fused if fits else plain
+    return body(grad_out, saved_input, keep_bits, gain)
+
+
 def solution(mesh):
     placed = (P("aa", "ba"), P(("aa", "ba"), None), P(("aa", "ba"), None), P())
     return jax.shard_map(

time: 63.6 us -> 30.9 us (0.49)
  blocking collectives: 34.2 us -> 0 us
  Pallas kernels: 0 us -> 27.3 us
  waiting for transfers between devices: 12.4 us -> 0 us
  starting transfers between devices: 5.33 us -> 0 us
  other arithmetic: 4.78 us -> 0 us
  local copies, waits for them, and re-layouts: 5.13 us -> 2.87 us
  between operations: 1.38 us -> 0.65 us
    pallas_call x0 -> x1, Pallas kernels: none -> 27.3 us  [fused(): pl.pallas_call(functools.partial(kernel, n_ba, n_aa), out_shape=(jax.Shap...]
    unnamed x1 -> x0, blocking collectives: 22.3 us -> none
    all_to_all x1 -> x0, waiting for transfers between devices: 12.4 us -> none  [per_device(): lax.all_to_all(pieces, 'ba', split_axis=0, concat_axis=2, tiled=True)]
    psum x1 -> x0, blocking collectives: 11.9 us -> none  [per_device(): share = lax.psum(owned, 'aa')]
    all_to_all x1 -> x0, starting transfers between devices: 5.33 us -> none  [per_device(): lax.all_to_all(pieces, 'ba', split_axis=0, concat_axis=2, tiled=True)]
    reduce_sum x2 -> x0, other arithmetic: 2.75 us -> none  [the longest x1 2.02 us: rows_backward(): partial_sum = jnp.sum(grads * normed, axis=0)]
    reshape x1 -> x0, local copies, waits for them, and re-layouts: 2.26 us -> none  [per_device(): pieces = grad_out.reshape(groups, rows, grad_out.shape[1])]
    convert_element_type x1 -> x0, other arithmetic: 1.43 us -> none  [rows_backward(): (inverse * (scaled - normed * centre) * keep * (1.0 / KEEP_RATE)).astype(...]
  transfers between devices with their start and end apart: 1 -> 0, of which waited for: 1 -> 0; matrix products, arithmetic and copies ran while one was open for 3% -> 0% of each run, Pallas kernels for 0% -> 0%
where the time goes in v1:
time: 30.9 us; the launch traced here: 30.8 us
  Pallas kernels  27.3 us (88%)
  local copies, waits for them, and re-layouts  2.87 us (9%)
  between operations  0.65 us (2%)
    pallas_call x1, Pallas kernels, fused(): pl.pallas_call(functools.partial(kernel, n_ba, n_aa), out_shape=(jax.Shap...  27.3 us
    unnamed x4, local copies, waits for them, and re-layouts  2.87 us

profile of v1, /device:TPU:0, one launch (start us, length us, event | category | flops | bytes accessed | tf_op | source)
XLA Modules:
  0.0 30.8 jit_solution(2227412844465671457)
XLA Ops:
  0.6 27.3 %regroup_backward.1 = (bf16[128,4096]{1,0:T(8,128)(2,1)}, f32[1,512]{1,0:T(1,128)}) custom-call(bf16[1024,512]{1,0:T(8,128)(2,1)} %grad_hbm.1, bf16[128,4096]{1,0:T(8,128)(2,1)} %input_hbm.1, s32[128,128]{1,0:T(8,128)} %bits_hbm.1, f32[1,4096]{1,0:T(1,128)} %bitcast.2), custom_call_target="tpu_custom_call" | custom-call | tf_op jit(solution)/shard_map/regroup_backward/pallas_call | solution.py:249
  27.9 0.0 copy-start
  27.9 2.3 %copy.8 = bf16[128,4096]{1,0:T(8,128)(2,1)} copy(bf16[128,4096]{1,0:T(8,128)(2,1)} %get-tuple-element.8) | data formatting | bytes 2097152
  30.2 0.0 copy-done
  30.2 0.6 %copy.9 = f32[512]{0:T(512)} copy(f32[512]{0:T(512)S(1)} %bitcast.3) | data formatting | bytes 4096
Async XLA Ops:
  27.9 2.3 %copy-start = (f32[1,512]{1,0:T(1,128)S(1)}, f32[1,512]{1,0:T(1,128)}, u32[]{:S(2)}) copy-start(f32[1,512]{1,0:T(1,128)} %get-tuple-element.5) | copy-start | bytes 6148

commit v2 on v1

--- a/solution.py
+++ b/solution.py
@@ -12,6 +12,7 @@
 EPSILON = 1e-06
 LANES = 128
 CHUNK_ROWS = 32
+STORES = 4
 MESH = pl.DeviceIdType.MESH
 
 
@@ -240,6 +241,18 @@
         share(step, aa).wait_send()
 
 
+def store(grad_vmem, share_vmem, grad_hbm, share_hbm, sem):
+    rows = grad_vmem.shape[0] // STORES
+    copies = [pltpu.make_async_copy(share_vmem, share_hbm, sem.at[STORES])]
+    for index in range(STORES):
+        block = pl.ds(index * rows, rows)
+        copies.append(pltpu.make_async_copy(grad_vmem.at[block], grad_hbm.at[block], sem.at[index]))
+    for copy in copies:
+        copy.start()
+    for copy in copies:
+        copy.wait()
+
+
 def fused(grad_out, saved_input, keep_bits, gain):
     n_ba, n_aa = lax.axis_size("ba"), lax.axis_size("aa")
     width = grad_out.shape[1]
@@ -249,8 +262,8 @@
     grad_in, share = pl.pallas_call(
         functools.partial(kernel, n_ba, n_aa),
         out_shape=(
-            jax.ShapeDtypeStruct((rows, depth), jnp.bfloat16),
-            jax.ShapeDtypeStruct((1, width), f32),
+            pltpu.VMEM((rows, depth), jnp.bfloat16),
+            pltpu.VMEM((1, width), f32),
         ),
         in_specs=[pl.BlockSpec(memory_space=pl.ANY)] * 4,
         out_specs=(pl.BlockSpec(memory_space=pltpu.VMEM), pl.BlockSpec(memory_space=pltpu.VMEM)),
@@ -278,6 +291,17 @@
         compiler_params=pltpu.CompilerParams(collective_id=0, has_side_effects=True),
         name="regroup_backward",
     )(grad_out, saved_input, keep_bits, gain.reshape(1, depth))
+    grad_in, share = pl.pallas_call(
+        store,
+        out_shape=(
+            jax.ShapeDtypeStruct((rows, depth), jnp.bfloat16),
+            jax.ShapeDtypeStruct((1, width), f32),
+        ),
+        in_specs=[pl.BlockSpec(memory_space=pltpu.VMEM)] * 2,
+        out_specs=[pl.BlockSpec(memory_space=pl.ANY)] * 2,
+        scratch_shapes=[pltpu.SemaphoreType.DMA((STORES + 1,))],
+        name="store_results",
+    )(*(pltpu.with_memory_space_constraint(x, pltpu.VMEM) for x in (grad_in, share)))
     return (grad_in, share.reshape(width))
 
 

time: 30.9 us -> 28.1 us (0.909)
  local copies, waits for them, and re-layouts: 2.87 us -> 0 us
    unnamed x4 -> x0, local copies, waits for them, and re-layouts: 2.87 us -> none
    pallas_call x1 -> x2, Pallas kernels: 27.3 us -> 27.3 us  [the longest x1 26.3 us: fused(): pl.pallas_call(functools.partial(kernel, n_ba, n_aa), out_shape=(pltpu.VM...]
where the time goes in v2:
time: 28.1 us; the launch traced here: 27.9 us
  Pallas kernels  27.3 us (97%)
  between operations  0.64 us (2%)
    pallas_call x1, Pallas kernels, fused(): pl.pallas_call(functools.partial(kernel, n_ba, n_aa), out_shape=(pltpu.VM...  26.3 us
    pallas_call x1, Pallas kernels, fused(): pl.pallas_call(store, out_shape=(jax.ShapeDtypeStruct((rows, depth), jnp....  1.01 us

profile of v2, /device:TPU:0, one launch (start us, length us, event | category | flops | bytes accessed | tf_op | source)
XLA Modules:
  0.0 27.9 jit_solution(18257551109384765232)
XLA Ops:
  0.6 26.3 %regroup_backward.1 = (bf16[128,4096]{1,0:T(8,128)(2,1)S(1)}, f32[1,512]{1,0:T(1,128)S(1)}) custom-call(bf16[1024,512]{1,0:T(8,128)(2,1)} %grad_hbm.1, bf16[128,4096]{1,0:T(8,128)(2,1)} %input_hbm.1, s32[128,128]{1,0:T(8,128)} %bits_hbm.1, f32[1,4096]{1,0:T(1,128)} %bitcast.2), custom_call_target="tpu_custom_call" | custom-call | tf_op jit(solution)/shard_map/regroup_backward/pallas_call | solution.py:262
  26.9 1.0 %store_results.1 = (bf16[128,4096]{1,0:T(8,128)(2,1)}, f32[1,512]{1,0:T(1,128)}) custom-call(bf16[128,4096]{1,0:T(8,128)(2,1)S(1)} %get-tuple-element.6.grad_vmem, f32[1,512]{1,0:T(1,128)S(1)} %get-tuple-element.7.share_vmem), custom_call_target="tpu_custom_call" | custom-call | tf_op jit(solution)/shard_map/store_results/pallas_call | solution.py:294

commit v3 on v2

v3 whole, which is shorter than its diff:
```python
import functools
import math

import jax
import jax.numpy as jnp
from jax import lax
from jax.experimental import pallas as pl
from jax.experimental.pallas import tpu as pltpu
from jax.sharding import PartitionSpec as P

KEEP_RATE = 0.9
EPSILON = 1e-06
LANES = 128
CHUNK_ROWS = 32
STORES = 4
MESH = pl.DeviceIdType.MESH


def unpack_bits(words):
    shifts = jnp.arange(32, dtype=jnp.int32)
    bits = jnp.right_shift(words[:, :, None], shifts[None, None, :]) & 1
    return bits.reshape(words.shape[0], words.shape[1] * 32).astype(jnp.float32)


def rows_backward(grad_rows, input_rows, word_rows, gain):
    keep = unpack_bits(word_rows)
    dropped = input_rows.astype(jnp.float32) * keep * (1.0 / KEEP_RATE)
    inverse = lax.rsqrt(jnp.mean(dropped * dropped, axis=-1, keepdims=True) + EPSILON)
    normed = dropped * inverse
    grads = grad_rows.astype(jnp.float32)
    scaled = gain[None, :] * grads
    centre = jnp.mean(scaled * normed, axis=-1, keepdims=True)
    grad_in = (inverse * (scaled - normed * centre) * keep * (1.0 / KEEP_RATE)).astype(jnp.bfloat16)
    partial_sum = jnp.sum(grads * normed, axis=0)
    return (grad_in, partial_sum)


def plain(grad_out, saved_input, keep_bits, gain):
    groups = lax.axis_size("ba")
    rows = grad_out.shape[0] // groups
    pieces = grad_out.reshape(groups, rows, grad_out.shape[1])
    arrived = lax.all_to_all(pieces, "ba", split_axis=0, concat_axis=2, tiled=True)
    grad_rows = arrived.reshape(rows, arrived.shape[2])
    grad_in, partial_sum = rows_backward(grad_rows, saved_input, keep_bits, gain)
    total_tokens = rows * groups * lax.axis_size("aa")
    owned = lax.psum_scatter(partial_sum, "ba", scatter_dimension=0, tiled=True)
    share = lax.psum(owned, "aa")
    gain_grad = share * (1.0 / math.sqrt(total_tokens))
    return (grad_in, gain_grad)


def far_count(n_ba):
    return max(1, n_ba // 4)


def kernel(n_ba, n_aa, grad_hbm, input_hbm, bits_hbm, gain_hbm, out_ref, share_ref,
           staged, arrived, held, words, gain_ref, normed, masked_gain, outer, totals, sums,
           parts, slices, shares, far_shares, stage_sem, load_sem, near_send, near_recv,
           far_send, far_recv, part_send, part_recv, share_send, share_recv,
           late_send, late_recv, ready):
    ba, aa = lax.axis_index("ba"), lax.axis_index("aa")
    rows, width = arrived.shape[1], arrived.shape[2]
    depth = n_ba * width
    chunks = rows // CHUNK_ROWS
    tiles = width // LANES
    n_far = far_count(n_ba)
    far = list(range(n_ba - n_far, n_ba))
    near = list(range(1, n_ba - n_far))
    near_order = sorted(near, key=lambda step: (step == 1, step % 2))

    def column(step):
        return lax.rem(aa + step, n_aa)

    def column_source(step):
        return lax.rem(aa + n_aa - step, n_aa)

    def rows_of(chunk):
        start = chunk * CHUNK_ROWS
        if not isinstance(start, int):
            start = pl.multiple_of(start, CHUNK_ROWS)
        return pl.ds(start, CHUNK_ROWS)

    def stage(step):
        first = pl.ds(pl.multiple_of((ba ^ step) * rows, CHUNK_ROWS), rows)
        target = staged.at[step] if step else arrived.at[0]
        return pltpu.make_async_copy(grad_hbm.at[first], target, stage_sem.at[step])

    def near_piece(step):
        return pltpu.make_async_remote_copy(
            src_ref=staged.at[step], dst_ref=arrived.at[step],
            send_sem=near_send.at[step], recv_sem=near_recv.at[step],
            device_id={"ba": ba ^ step}, device_id_type=MESH,
        )

    def far_piece(chunk, index):
        step, block = far[index], rows_of(chunk)
        return pltpu.make_async_remote_copy(
            src_ref=staged.at[step, block], dst_ref=arrived.at[step, block],
            send_sem=far_send.at[chunk, index], recv_sem=far_recv.at[chunk, index],
            device_id={"ba": ba ^ step}, device_id_type=MESH,
        )

    def part(step):
        return pltpu.make_async_remote_copy(
            src_ref=parts.at[step], dst_ref=slices.at[step],
            send_sem=part_send.at[step], recv_sem=part_recv.at[step],
            device_id={"ba": ba ^ step}, device_id_type=MESH,
        )

    def share(step, slot):
        return pltpu.make_async_remote_copy(
            src_ref=shares.at[aa], dst_ref=shares.at[slot],
            send_sem=share_send.at[step], recv_sem=share_recv.at[step],
            device_id={"aa": column(step)}, device_id_type=MESH,
        )

    def late(step, index, slot):
        return pltpu.make_async_remote_copy(
            src_ref=parts.at[far[index]], dst_ref=far_shares.at[slot, index],
            send_sem=late_send.at[step, index], recv_sem=late_recv.at[step, index],
            device_id={"aa": column(step), "ba": ba ^ far[index]}, device_id_type=MESH,
        )

    barrier = pltpu.get_barrier_semaphore()
    for step in range(1, n_ba):
        pl.semaphore_signal(barrier, inc=1, device_id={"ba": ba ^ step}, device_id_type=MESH)
    for step in range(1, n_aa):
        pl.semaphore_signal(barrier, inc=1, device_id={"aa": column(step)}, device_id_type=MESH)
    for step in near_order:
        stage(step).start()
    loads = [
        pltpu.make_async_copy(bits_hbm, words, load_sem.at[0]),
        pltpu.make_async_copy(gain_hbm, gain_ref, load_sem.at[1]),
        pltpu.make_async_copy(input_hbm, held, load_sem.at[2]),
    ]
    for load in loads:
        load.start()
    for step in far + [0]:
        stage(step).start()
    pl.semaphore_wait(barrier, n_ba + n_aa - 2)
    for step in near_order:
        stage(step).wait()
        near_piece(step).start()
    for step in far:
        pl.semaphore_signal(ready, inc=1, device_id={"ba": ba ^ step}, device_id_type=MESH)
        stage(step).wait()
    ahead = chunks // 2
    for chunk in range(ahead):
        for index in range(n_far):
            far_piece(chunk, index).start()
    for load in loads:
        load.wait()

    lane = lax.broadcasted_iota(jnp.int32, (CHUNK_ROWS, LANES), 1)
    word_of = lane // 32
    flag = jnp.left_shift(jnp.int32(1), lane % 32)

    def span(source, tile):
        return pl.ds(pl.multiple_of(source * width + tile * LANES, LANES), LANES)

    def prepare(chunk, carry):
        block = rows_of(chunk)

        def drop(source, squares):
            row_words = words[block, :]
            for tile in range(tiles):
                at = span(source, tile)
                index = word_of + (source * tiles + tile) * (LANES // 32)
                spread = jnp.take_along_axis(row_words, index, axis=1, mode="promise_in_bounds")
                kept = (spread & flag) != 0
                dropped = jnp.where(kept, held[block, at].astype(jnp.float32), 0.0) * (1.0 / KEEP_RATE)
                normed[block, at] = dropped
                masked_gain[block, at] = jnp.where(kept, gain_ref[:, at], 0.0)
                squares = squares + dropped * dropped
            return squares

        squares = lax.fori_loop(0, n_ba, drop, jnp.zeros((CHUNK_ROWS, LANES), jnp.float32))
        mean = jnp.sum(squares, axis=1, keepdims=True) * (1.0 / depth)
        inverse = lax.rsqrt(mean + EPSILON)
        outer[block, :] = jnp.broadcast_to(inverse * (1.0 / KEEP_RATE), (CHUNK_ROWS, LANES))

        def scale(source, none):
            for tile in range(tiles):
                at = span(source, tile)
                normed[block, at] = normed[block, at] * inverse
            return none

        lax.fori_loop(0, n_ba, scale, 0)
        return carry

    lax.fori_loop(0, chunks, prepare, 0)
    sums[...] = jnp.zeros_like(sums)
    totals[...] = jnp.zeros_like(totals)

    def first(step, chunk):
        block, source = rows_of(chunk), ba ^ step
        total = totals[block, :]
        for tile in range(tiles):
            at = span(source, tile)
            here = slice(tile * LANES, (tile + 1) * LANES)
            grads = arrived[step, block, here].astype(jnp.float32)
            product = grads * normed[block, at]
            total = total + product * gain_ref[:, at]
            sums[step, :, here] += jnp.sum(product.reshape(CHUNK_ROWS // 8, 8, LANES), axis=0)
        totals[block, :] = total

    def finish(chunk):
        block = rows_of(chunk)
        factor = outer[block, :]
        centre = jnp.sum(totals[block, :], axis=1, keepdims=True) * (1.0 / depth)

        def last(step, none):
            for tile in range(tiles):
                at = span(ba ^ step, tile)
                grads = arrived[step, block, tile * LANES:(tile + 1) * LANES].astype(jnp.float32)
                value = factor * (masked_gain[block, at] * grads - normed[block, at] * centre)
                out_ref[block, at] = value.astype(jnp.bfloat16)
            return none

        lax.fori_loop(0, n_ba, last, 0)

    def fold(step):
        return jnp.sum(sums[step], axis=0, keepdims=True)

    for step in [0] + sorted(near, key=lambda step: (step != 1, step % 2)):
        if step:
            near_piece(step).wait_recv()
        else:
            stage(0).wait()

        def whole(chunk, none, step=step):
            first(step, chunk)
            return none

        lax.fori_loop(0, chunks, whole, 0)
        if step:
            parts[step] = fold(step)
        else:
            slices[0] = fold(0)
    for step in reversed(near):
        part(step).start()
    for chunk in range(ahead, chunks):
        for index in range(n_far):
            far_piece(chunk, index).start()

    def gather_near():
        total = slices[0]
        for step in near:
            part(step).wait_recv()
            total = total + slices[step]
        shares[aa] = total
        for step in range(1, n_aa):
            share(step, aa).start()

    for chunk in range(chunks):
        if chunk == chunks - 1:
            gather_near()
        for index in range(n_far):
            far_piece(chunk, index).wait_recv()
            first(far[index], chunk)
        if chunk < chunks - 1:
            finish(chunk)
    for step in far:
        parts[step] = fold(step)
    pl.semaphore_wait(ready, n_far)
    for step in reversed(range(n_aa)):
        for index in range(n_far):
            late(step, index, aa).start()
    finish(chunks - 1)
    for step in near:
        near_piece(step).wait_send()
        part(step).wait_send()
    for chunk in range(chunks):
        for index in range(n_far):
            far_piece(chunk, index).wait_send()
    for step in range(1, n_aa):
        share(step, column_source(step)).wait_recv()
    for step in range(n_aa):
        for index in range(n_far):
            late(step, index, column_source(step)).wait_recv()
    total = jnp.zeros((1, width), jnp.float32)
    for source in range(n_aa):
        total = total + shares[source]
        for index in range(n_far):
            total = total + far_shares[source, index]
    share_ref[...] = total * (1.0 / math.sqrt(rows * n_ba * n_aa))
    for step in range(1, n_aa):
        share(step, aa).wait_send()
    for step in range(n_aa):
        for index in range(n_far):
            late(step, index, aa).wait_send()


def store(grad_vmem, share_vmem, grad_hbm, share_hbm, sem):
    rows = grad_vmem.shape[0] // STORES
    copies = [pltpu.make_async_copy(share_vmem, share_hbm, sem.at[STORES])]
    for index in range(STORES):
        block = pl.ds(index * rows, rows)
        copies.append(pltpu.make_async_copy(grad_vmem.at[block], grad_hbm.at[block], sem.at[index]))
    for copy in copies:
        copy.start()
    for copy in copies:
        copy.wait()


def fused(grad_out, saved_input, keep_bits, gain):
    n_ba, n_aa = lax.axis_size("ba"), lax.axis_size("aa")
    width = grad_out.shape[1]
    rows, depth = saved_input.shape
    chunks, n_far = rows // CHUNK_ROWS, far_count(n_ba)
    f32 = jnp.float32
    grad_in, share = pl.pallas_call(
        functools.partial(kernel, n_ba, n_aa),
        out_shape=(
            pltpu.VMEM((rows, depth), jnp.bfloat16),
            pltpu.VMEM((1, width), f32),
        ),
        in_specs=[pl.BlockSpec(memory_space=pl.ANY)] * 4,
        out_specs=(pl.BlockSpec(memory_space=pltpu.VMEM), pl.BlockSpec(memory_space=pltpu.VMEM)),
        scratch_shapes=[
            pltpu.VMEM((n_ba, rows, width), jnp.bfloat16),
            pltpu.VMEM((n_ba, rows, width), jnp.bfloat16),
            pltpu.VMEM((rows, depth), jnp.bfloat16),
            pltpu.VMEM(keep_bits.shape, jnp.int32),
            pltpu.VMEM((1, depth), f32),
            pltpu.VMEM((rows, depth), f32),
            pltpu.VMEM((rows, depth), f32),
            pltpu.VMEM((rows, LANES), f32),
            pltpu.VMEM((rows, LANES), f32),
            pltpu.VMEM((n_ba, 8, width), f32),
            pltpu.VMEM((n_ba, 1, width), f32),
            pltpu.VMEM((n_ba, 1, width), f32),
            pltpu.VMEM((n_aa, 1, width), f32),
            pltpu.VMEM((n_aa, n_far, 1, width), f32),
            pltpu.SemaphoreType.DMA((n_ba,)),
            pltpu.SemaphoreType.DMA((3,)),
            pltpu.SemaphoreType.DMA((n_ba,)),
            pltpu.SemaphoreType.DMA((n_ba,)),
            pltpu.SemaphoreType.DMA((chunks, n_far)),
            pltpu.SemaphoreType.DMA((chunks, n_far)),
            pltpu.SemaphoreType.DMA((n_ba,)),
            pltpu.SemaphoreType.DMA((n_ba,)),
            pltpu.SemaphoreType.DMA((n_aa,)),
            pltpu.SemaphoreType.DMA((n_aa,)),
            pltpu.SemaphoreType.DMA((n_aa, n_far)),
            pltpu.SemaphoreType.DMA((n_aa, n_far)),
            pltpu.SemaphoreType.REGULAR,
        ],
        compiler_params=pltpu.CompilerParams(collective_id=0, has_side_effects=True),
        name="regroup_backward",
    )(grad_out, saved_input, keep_bits, gain.reshape(1, depth))
    grad_in, share = pl.pallas_call(
        store,
        out_shape=(
            jax.ShapeDtypeStruct((rows, depth), jnp.bfloat16),
            jax.ShapeDtypeStruct((1, width), f32),
        ),
        in_specs=[pl.BlockSpec(memory_space=pltpu.VMEM)] * 2,
        out_specs=[pl.BlockSpec(memory_space=pl.ANY)] * 2,
        scratch_shapes=[pltpu.SemaphoreType.DMA((STORES + 1,))],
        name="store_results",
    )(*(pltpu.with_memory_space_constraint(x, pltpu.VMEM) for x in (grad_in, share)))
    return (grad_in, share.reshape(width))


def per_device(grad_out, saved_input, keep_bits, gain):
    fits = grad_out.shape[1] % LANES == 0 and saved_input.shape[0] % CHUNK_ROWS == 0
    fits = fits and keep_bits.shape[1] == LANES
    n_ba = lax.axis_size("ba")
    fits = fits and n_ba > 1 and n_ba & (n_ba - 1) == 0
    body = fused if fits else plain
    return body(grad_out, saved_input, keep_bits, gain)


def solution(mesh):
    placed = (P("aa", "ba"), P(("aa", "ba"), None), P(("aa", "ba"), None), P())
    return jax.shard_map(
        per_device,
        mesh=mesh,
        in_specs=placed,
        out_specs=(P(("aa", "ba"), None), P("ba")),
        check_vma=False,
    )
```

time: 28.1 us -> 26.2 us (0.932)
  Pallas kernels: 27.3 us -> 25.4 us
    pallas_call x1, Pallas kernels: 26.3 us -> 24.4 us  [fused(): pl.pallas_call(functools.partial(kernel, n_ba, n_aa), out_shape=(pltpu.VM...]
where the time goes in v3:
time: 26.2 us; the launch traced here: 26 us
  Pallas kernels  25.4 us (97%)
  between operations  0.64 us (2%)
    pallas_call x1, Pallas kernels, fused(): pl.pallas_call(functools.partial(kernel, n_ba, n_aa), out_shape=(pltpu.VM...  24.4 us
    pallas_call x1, Pallas kernels, fused(): pl.pallas_call(store, out_shape=(jax.ShapeDtypeStruct((rows, depth), jnp....  1.01 us

profile of v3, /device:TPU:0, one launch (start us, length us, event | category | flops | bytes accessed | tf_op | source)
XLA Modules:
  0.0 26.0 jit_solution(17710349210882010815)
XLA Ops:
  0.6 24.4 %regroup_backward.1 = (bf16[128,4096]{1,0:T(8,128)(2,1)S(1)}, f32[1,512]{1,0:T(1,128)S(1)}) custom-call(bf16[1024,512]{1,0:T(8,128)(2,1)} %grad_hbm.1, bf16[128,4096]{1,0:T(8,128)(2,1)} %input_hbm.1, s32[128,128]{1,0:T(8,128)} %bits_hbm.1, f32[1,4096]{1,0:T(1,128)} %bitcast.2), custom_call_target="tpu_custom_call" | custom-call | tf_op jit(solution)/shard_map/regroup_backward/pallas_call | solution.py:312
  25.0 1.0 %store_results.1 = (bf16[128,4096]{1,0:T(8,128)(2,1)}, f32[1,512]{1,0:T(1,128)}) custom-call(bf16[128,4096]{1,0:T(8,128)(2,1)S(1)} %get-tuple-element.6.grad_vmem, f32[1,512]{1,0:T(1,128)S(1)} %get-tuple-element.7.share_vmem), custom_call_target="tpu_custom_call" | custom-call | tf_op jit(solution)/shard_map/store_results/pallas_call | solution.py:352

commit v4 on v3

--- a/solution.py
+++ b/solution.py
@@ -49,8 +49,8 @@
     return (grad_in, gain_grad)
 
 
-def far_count(n_ba):
-    return max(1, n_ba // 4)
+def late_steps(n_ba):
+    return list(range(max(1, n_ba // 4), n_ba - n_ba // 4))
 
 
 def kernel(n_ba, n_aa, grad_hbm, input_hbm, bits_hbm, gain_hbm, out_ref, share_ref,
@@ -63,10 +63,11 @@
     depth = n_ba * width
     chunks = rows // CHUNK_ROWS
     tiles = width // LANES
-    n_far = far_count(n_ba)
-    far = list(range(n_ba - n_far, n_ba))
-    near = list(range(1, n_ba - n_far))
-    near_order = sorted(near, key=lambda step: (step == 1, step % 2))
+    far = late_steps(n_ba)
+    far = sorted(far, key=lambda step: step % 2)
+    n_far = len(far)
+    near = [step for step in range(1, n_ba) if step not in far]
+    near_order = sorted(near, reverse=True)
 
     def column(step):
         return lax.rem(aa + step, n_aa)
@@ -144,10 +145,6 @@
     for step in far:
         pl.semaphore_signal(ready, inc=1, device_id={"ba": ba ^ step}, device_id_type=MESH)
         stage(step).wait()
-    ahead = chunks // 2
-    for chunk in range(ahead):
-        for index in range(n_far):
-            far_piece(chunk, index).start()
     for load in loads:
         load.wait()
 
@@ -191,6 +188,12 @@
     lax.fori_loop(0, chunks, prepare, 0)
     sums[...] = jnp.zeros_like(sums)
     totals[...] = jnp.zeros_like(totals)
+    for step in near:
+        near_piece(step).wait_send()
+    ahead = chunks // 2
+    for chunk in range(ahead):
+        for index in range(n_far):
+            far_piece(chunk, index).start()
 
     def first(step, chunk):
         block, source = rows_of(chunk), ba ^ step
@@ -222,7 +225,7 @@
     def fold(step):
         return jnp.sum(sums[step], axis=0, keepdims=True)
 
-    for step in [0] + sorted(near, key=lambda step: (step != 1, step % 2)):
+    for step in [0] + near:
         if step:
             near_piece(step).wait_recv()
         else:
@@ -268,7 +271,6 @@
             late(step, index, aa).start()
     finish(chunks - 1)
     for step in near:
-        near_piece(step).wait_send()
         part(step).wait_send()
     for chunk in range(chunks):
         for index in range(n_far):
@@ -307,7 +309,7 @@
     n_ba, n_aa = lax.axis_size("ba"), lax.axis_size("aa")
     width = grad_out.shape[1]
     rows, depth = saved_input.shape
-    chunks, n_far = rows // CHUNK_ROWS, far_count(n_ba)
+    chunks, n_far = rows // CHUNK_ROWS, len(late_steps(n_ba))
     f32 = jnp.float32
     grad_in, share = pl.pallas_call(
         functools.partial(kernel, n_ba, n_aa),

time: 26.2 us -> 25.7 us (0.981)
  Pallas kernels: 25.4 us -> 24.9 us
    pallas_call x1, Pallas kernels: 24.4 us -> 23.9 us  [fused(): pl.pallas_call(functools.partial(kernel, n_ba, n_aa), out_shape=(pltpu.VM...]
where the time goes in v4:
time: 25.7 us; the launch traced here: 25.6 us
  Pallas kernels  24.9 us (97%)
  between operations  0.64 us (2%)
    pallas_call x1, Pallas kernels, fused(): pl.pallas_call(functools.partial(kernel, n_ba, n_aa), out_shape=(pltpu.VM...  23.9 us
    pallas_call x1, Pallas kernels, fused(): pl.pallas_call(store, out_shape=(jax.ShapeDtypeStruct((rows, depth), jnp....  1.01 us

profile of v4, /device:TPU:0, one launch (start us, length us, event | category | flops | bytes accessed | tf_op | source)
XLA Modules:
  0.0 25.6 jit_solution(1681828578693255836)
XLA Ops:
  0.6 23.9 %regroup_backward.1 = (bf16[128,4096]{1,0:T(8,128)(2,1)S(1)}, f32[1,512]{1,0:T(1,128)S(1)}) custom-call(bf16[1024,512]{1,0:T(8,128)(2,1)} %grad_hbm.1, bf16[128,4096]{1,0:T(8,128)(2,1)} %input_hbm.1, s32[128,128]{1,0:T(8,128)} %bits_hbm.1, f32[1,4096]{1,0:T(1,128)} %bitcast.2), custom_call_target="tpu_custom_call" | custom-call | tf_op jit(solution)/shard_map/regroup_backward/pallas_call | solution.py:314
  24.6 1.0 %store_results.1 = (bf16[128,4096]{1,0:T(8,128)(2,1)}, f32[1,512]{1,0:T(1,128)}) custom-call(bf16[128,4096]{1,0:T(8,128)(2,1)S(1)} %get-tuple-element.6.grad_vmem, f32[1,512]{1,0:T(1,128)S(1)} %get-tuple-element.7.share_vmem), custom_call_target="tpu_custom_call" | custom-call | tf_op jit(solution)/shard_map/store_results/pallas_call | solution.py:354

commit v5 on v4

--- a/solution.py
+++ b/solution.py
@@ -11,7 +11,7 @@
 KEEP_RATE = 0.9
 EPSILON = 1e-06
 LANES = 128
-CHUNK_ROWS = 32
+CHUNK_ROWS = 64
 STORES = 4
 MESH = pl.DeviceIdType.MESH
 

time: 25.7 us -> 25.3 us (0.984)
  Pallas kernels: 24.9 us -> 24.5 us
    pallas_call x1, Pallas kernels: 23.9 us -> 23.5 us  [fused(): pl.pallas_call(functools.partial(kernel, n_ba, n_aa), out_shape=(pltpu.VM...]
where the time goes in v5:
time: 25.3 us; the launch traced here: 25.1 us
  Pallas kernels  24.5 us (97%)
  between operations  0.64 us (3%)
    pallas_call x1, Pallas kernels, fused(): pl.pallas_call(functools.partial(kernel, n_ba, n_aa), out_shape=(pltpu.VM...  23.5 us
    pallas_call x1, Pallas kernels, fused(): pl.pallas_call(store, out_shape=(jax.ShapeDtypeStruct((rows, depth), jnp....  1.01 us

profile of v5, /device:TPU:0, one launch (start us, length us, event | category | flops | bytes accessed | tf_op | source)
XLA Modules:
  0.0 25.1 jit_solution(5713802601842031932)
XLA Ops:
  0.6 23.5 %regroup_backward.1 = (bf16[128,4096]{1,0:T(8,128)(2,1)S(1)}, f32[1,512]{1,0:T(1,128)S(1)}) custom-call(bf16[1024,512]{1,0:T(8,128)(2,1)} %grad_hbm.1, bf16[128,4096]{1,0:T(8,128)(2,1)} %input_hbm.1, s32[128,128]{1,0:T(8,128)} %bits_hbm.1, f32[1,4096]{1,0:T(1,128)} %bitcast.2), custom_call_target="tpu_custom_call" | custom-call | tf_op jit(solution)/shard_map/regroup_backward/pallas_call | solution.py:314
  24.1 1.0 %store_results.1 = (bf16[128,4096]{1,0:T(8,128)(2,1)}, f32[1,512]{1,0:T(1,128)}) custom-call(bf16[128,4096]{1,0:T(8,128)(2,1)S(1)} %get-tuple-element.6.grad_vmem, f32[1,512]{1,0:T(1,128)S(1)} %get-tuple-element.7.share_vmem), custom_call_target="tpu_custom_call" | custom-call | tf_op jit(solution)/shard_map/store_results/pallas_call | solution.py:354
